TPU v7x, 32 devices: a whole 2x2x4 slice. The times are simulated.
32 devices in a mesh: wide: 8 (over y, x, core), head: 4 (over z).
Axes of the slice: x: 2, y: 2, z: 4, core: 2. Of those that a mesh axis runs over, the one named last changes fastest.
Arguments:
- tokens: bfloat16 [16384, 1024], P(('wide', 'head')), may hold values from -6 to 6
- cotangent: bfloat16 [16384, 1024], P(('wide', 'head')), may hold values from -6 to 6
- w_query: bfloat16 [1024, 1024], P('wide', 'head'), may hold values from -0.25 to 0.25
- w_key: bfloat16 [1024, 1024], P('wide', 'head'), may hold values from -0.25 to 0.25
- w_value: bfloat16 [1024, 1024], P('wide', 'head'), may hold values from -0.1875 to 0.1875
- w_out: bfloat16 [1024, 1024], P('head', 'wide'), may hold values from -0.1875 to 0.1875
- w_up: bfloat16 [1024, 4096], P('wide', 'head'), may hold values from -0.1875 to 0.1875
- w_down: bfloat16 [4096, 1024], P('head', 'wide'), may hold values from -0.09375 to 0.09375
- norm_gain: float32 [4, 1024], replicated, may hold values from 0.25 to 1.75
- norm_bias: float32 [4, 1024], replicated, may hold values from -3 to 3
Outputs:
- block_out: bfloat16 [16384, 1024], P(('wide', 'head'))
- input_grad: float32 [16384, 1024], P(('wide', 'head'))
- grad_query: float32 [1024, 1024], P('wide', 'head')
- grad_key: float32 [1024, 1024], P('wide', 'head')
- grad_value: float32 [1024, 1024], P('wide', 'head')
- grad_out: float32 [1024, 1024], P('head', 'wide')
- grad_up: float32 [1024, 4096], P('wide', 'head')
- grad_down: float32 [4096, 1024], P('head', 'wide')
- gain_grad: float32 [4, 1024], replicated
- bias_grad: float32 [4, 1024], replicated
All inputs are finite; a program needn't handle non-finite values.
Results may differ from a plain program's by a relative error of at most 0.015.
Values may be sent and summed in bfloat16 or wider, within the bound.
No kernel may reach another device: no remote copies, remote signals or barrier semaphores. Data moves between devices by JAX's collectives and lax.ppermute only.
A program may use at most 192 MiB of HBM per device.

v0:
```python
import math
import jax
import jax.numpy as jnp
from jax import lax
from jax.sharding import PartitionSpec as P

HD = 64
EPS = 1e-05


def normalize(values, gain, bias):
    average = jnp.mean(values, axis=-1, keepdims=True)
    centred = values - average
    inverse = lax.rsqrt(jnp.mean(centred * centred, axis=-1, keepdims=True) + EPS)
    unit_rows = centred * inverse
    return (unit_rows * gain + bias, unit_rows, inverse)


def normalize_back(gradient, unit_rows, inverse, gain):
    scaled = gradient * gain
    inner_sum = (
        scaled
        - jnp.mean(scaled, axis=-1, keepdims=True)
        - unit_rows * jnp.mean(scaled * unit_rows, axis=-1, keepdims=True)
    )
    return (inner_sum * inverse, jnp.sum(gradient * unit_rows, axis=0), jnp.sum(gradient, axis=0))


def rows_in(values):
    return lax.all_gather(values, "head", axis=0, tiled=True)


def grads_in(values):
    return lax.all_gather(values, "head", axis=0, tiled=True)


def branch_sum(left_op, right_op):
    return lax.psum_scatter(
        jnp.dot(left_op, right_op, preferred_element_type=jnp.float32),
        "head",
        scatter_dimension=0,
        tiled=True,
    )


def input_sum(operand_pairs):
    summed = None
    for left_op, right_op in operand_pairs:
        partial_value = lax.dot_general(
            left_op, right_op, (((1,), (1,)), ((), ())), preferred_element_type=jnp.float32
        )
        summed = partial_value if summed is None else summed + partial_value
    return lax.psum_scatter(summed, "head", scatter_dimension=0, tiled=True)


def masked_scores(rows_q, key_heads, first_row, score_scale):
    scores = (
        jnp.einsum("qgd,kgd->gqk", rows_q, key_heads, preferred_element_type=jnp.float32)
        * score_scale
    )
    place_q = first_row + jnp.arange(rows_q.shape[0], dtype=jnp.int32)
    place_k = jnp.arange(key_heads.shape[0], dtype=jnp.int32)
    allowed = place_k[None, :] <= place_q[:, None]
    return jnp.where(allowed[None], scores, -1e30)


def attend(queries, key_rows, value_rows, block_rows):
    length, width = queries.shape
    groups = width // HD
    score_scale = 1.0 / math.sqrt(HD)
    query_heads = queries.reshape(length, groups, HD)
    key_heads = key_rows.reshape(length, groups, HD)
    value_heads = value_rows.reshape(length, groups, HD)
    out_blocks = []
    totals = []
    for position in range(length // block_rows):
        first_row = position * block_rows
        last_row = first_row + block_rows
        scores = masked_scores(
            query_heads[first_row:last_row], key_heads[:last_row], first_row, score_scale
        )
        row_max = jnp.max(scores, axis=-1, keepdims=True)
        exp_scores = jnp.exp(scores - row_max)
        row_total = jnp.sum(exp_scores, axis=-1, keepdims=True)
        weights = (exp_scores / row_total).astype(jnp.bfloat16)
        out_blocks.append(
            jnp.einsum(
                "gqk,kgd->qgd", weights, value_heads[:last_row], preferred_element_type=jnp.float32
            )
        )
        totals.append(row_max + jnp.log(row_total))
    return (jnp.concatenate(out_blocks, axis=0).reshape(length, width), totals)


def attend_back(queries, key_rows, value_rows, grad_rows, totals, block_rows):
    length, width = queries.shape
    groups = width // HD
    score_scale = 1.0 / math.sqrt(HD)
    query_heads = queries.reshape(length, groups, HD)
    key_heads = key_rows.reshape(length, groups, HD)
    value_heads = value_rows.reshape(length, groups, HD)
    grad_heads = grad_rows.reshape(length, groups, HD)
    grad_keys = jnp.zeros((length, groups, HD), jnp.float32)
    grad_values = jnp.zeros((length, groups, HD), jnp.float32)
    query_parts = []
    for position in range(length // block_rows):
        first_row = position * block_rows
        last_row = first_row + block_rows
        rows_q = query_heads[first_row:last_row]
        scores = masked_scores(rows_q, key_heads[:last_row], first_row, score_scale)
        weights = jnp.exp(scores - totals[position])
        rounded = weights.astype(jnp.bfloat16)
        grad_block = grad_heads[first_row:last_row]
        grad_values = grad_values.at[:last_row].add(
            jnp.einsum("gqk,qgd->kgd", rounded, grad_block, preferred_element_type=jnp.float32)
        )
        grad_weights = jnp.einsum(
            "qgd,kgd->gqk", grad_block, value_heads[:last_row], preferred_element_type=jnp.float32
        )
        inner_sum = jnp.sum(weights * grad_weights, axis=-1, keepdims=True)
        grad_scores = (weights * (grad_weights - inner_sum)).astype(jnp.bfloat16)
        query_parts.append(
            jnp.einsum(
                "gqk,kgd->qgd",
                grad_scores,
                key_heads[:last_row],
                preferred_element_type=jnp.float32,
            )
            * score_scale
        )
        grad_keys = grad_keys.at[:last_row].add(
            jnp.einsum("gqk,qgd->kgd", grad_scores, rows_q, preferred_element_type=jnp.float32)
            * score_scale
        )
    grad_queries = jnp.concatenate(query_parts, axis=0).reshape(length, width).astype(jnp.bfloat16)
    return (
        grad_queries,
        grad_keys.reshape(length, width).astype(jnp.bfloat16),
        grad_values.reshape(length, width).astype(jnp.bfloat16),
    )


def contract_rows(left_op, right_op):
    return lax.dot_general(
        left_op, right_op, (((0,), (0,)), ((), ())), preferred_element_type=jnp.float32
    )


def contract_cols(left_op, right_op):
    return lax.dot_general(
        left_op, right_op, (((1,), (1,)), ((), ())), preferred_element_type=jnp.float32
    )


def on_device(
    tokens, cotangent, w_query, w_key, w_value, w_out, w_up, w_down, norm_gain, norm_bias
):
    full_q, full_k, full_v, full_o, full_up, full_down = (
        lax.all_gather(w_query, "wide", axis=0, tiled=True),
        lax.all_gather(w_key, "wide", axis=0, tiled=True),
        lax.all_gather(w_value, "wide", axis=0, tiled=True),
        lax.all_gather(w_out, "wide", axis=1, tiled=True),
        lax.all_gather(w_up, "wide", axis=0, tiled=True),
        lax.all_gather(w_down, "wide", axis=1, tiled=True),
    )
    residual = tokens.astype(jnp.float32)
    norm_a, unit_a, inv_a = normalize(residual, norm_gain[0], norm_bias[0])
    seq_a = rows_in(norm_a.astype(jnp.bfloat16))
    block_rows = min(512, seq_a.shape[0])
    queries = jnp.dot(seq_a, full_q, preferred_element_type=jnp.float32).astype(jnp.bfloat16)
    key_rows = jnp.dot(seq_a, full_k, preferred_element_type=jnp.float32).astype(jnp.bfloat16)
    value_rows = jnp.dot(seq_a, full_v, preferred_element_type=jnp.float32).astype(jnp.bfloat16)
    attended, totals = attend(queries, key_rows, value_rows, block_rows)
    attended = attended.astype(jnp.bfloat16)
    mixed = branch_sum(attended, full_o)
    norm_z, unit_z, inv_z = normalize(mixed, norm_gain[1], norm_bias[1])
    hidden = residual + norm_z
    norm_c, unit_c, inv_c = normalize(hidden, norm_gain[2], norm_bias[2])
    seq_c = rows_in(norm_c.astype(jnp.bfloat16))
    pre_act = jnp.dot(seq_c, full_up, preferred_element_type=jnp.float32)
    active, gelu_back = jax.vjp(jax.nn.gelu, pre_act)
    active = active.astype(jnp.bfloat16)
    output = branch_sum(active, full_down)
    norm_m, unit_m, inv_m = normalize(output, norm_gain[3], norm_bias[3])
    block_out = (hidden + norm_m).astype(jnp.bfloat16)
    full_q, full_k, full_v, full_o, full_up, full_down = (
        lax.all_gather(w_query, "wide", axis=0, tiled=True),
        lax.all_gather(w_key, "wide", axis=0, tiled=True),
        lax.all_gather(w_value, "wide", axis=0, tiled=True),
        lax.all_gather(w_out, "wide", axis=1, tiled=True),
        lax.all_gather(w_up, "wide", axis=0, tiled=True),
        lax.all_gather(w_down, "wide", axis=1, tiled=True),
    )
    grad_y = cotangent.astype(jnp.float32)
    grad_m, gain_m, bias_m = normalize_back(grad_y, unit_m, inv_m, norm_gain[3])
    seq_gm = grads_in(grad_m.astype(jnp.bfloat16))
    grad_act = contract_cols(seq_gm, full_down)
    grad_pre = gelu_back(grad_act)[0].astype(jnp.bfloat16)
    grad_down = contract_rows(active, seq_gm)
    grad_up = contract_rows(seq_c, grad_pre)
    grad_c = input_sum(((grad_pre, full_up),))
    grad_more, gain_c, bias_c = normalize_back(grad_c, unit_c, inv_c, norm_gain[2])
    grad_h = grad_y + grad_more
    grad_z, gain_z, bias_z = normalize_back(grad_h, unit_z, inv_z, norm_gain[1])
    seq_gz = grads_in(grad_z.astype(jnp.bfloat16))
    grad_att = contract_cols(seq_gz, full_o).astype(jnp.bfloat16)
    grad_o = contract_rows(attended, seq_gz)
    grad_queries, grad_keys, grad_values = attend_back(
        queries, key_rows, value_rows, grad_att, totals, block_rows
    )
    grad_q = contract_rows(seq_a, grad_queries)
    grad_k = contract_rows(seq_a, grad_keys)
    grad_v = contract_rows(seq_a, grad_values)
    grad_a = input_sum(((grad_queries, full_q), (grad_keys, full_k), (grad_values, full_v)))
    grad_first, gain_a, bias_a = normalize_back(grad_a, unit_a, inv_a, norm_gain[0])
    input_grad = grad_h + grad_first
    grad_q, grad_k, grad_v, grad_o, grad_up, grad_down = (
        lax.psum_scatter(grad_q, "wide", scatter_dimension=0, tiled=True),
        lax.psum_scatter(grad_k, "wide", scatter_dimension=0, tiled=True),
        lax.psum_scatter(grad_v, "wide", scatter_dimension=0, tiled=True),
        lax.psum_scatter(grad_o, "wide", scatter_dimension=1, tiled=True),
        lax.psum_scatter(grad_up, "wide", scatter_dimension=0, tiled=True),
        lax.psum_scatter(grad_down, "wide", scatter_dimension=1, tiled=True),
    )
    gain_grad, bias_grad = lax.psum(
        (jnp.stack([gain_a, gain_z, gain_c, gain_m]), jnp.stack([bias_a, bias_z, bias_c, bias_m])),
        ("wide", "head"),
    )
    return (
        block_out,
        input_grad,
        grad_q,
        grad_k,
        grad_v,
        grad_o,
        grad_up,
        grad_down,
        gain_grad,
        bias_grad,
    )


def solution(mesh):
    in_specs = (
        P(("wide", "head"), None),
        P(("wide", "head"), None),
        P("wide", "head"),
        P("wide", "head"),
        P("wide", "head"),
        P("head", "wide"),
        P("wide", "head"),
        P("head", "wide"),
        P(),
        P(),
    )
    out_specs = (
        P(("wide", "head"), None),
        P(("wide", "head"), None),
        P("wide", "head"),
        P("wide", "head"),
        P("wide", "head"),
        P("head", "wide"),
        P("wide", "head"),
        P("head", "wide"),
        P(),
        P(),
    )
    return jax.shard_map(
        on_device, mesh=mesh, in_specs=in_specs, out_specs=out_specs, check_vma=False
    )
```

profile of v0, /device:TPU:0, one launch (start us, length us, event | category | flops | bytes accessed | tf_op | source)
XLA Modules:
  0.0 1443.2 jit_solution(8579794204711242059)
XLA Ops:
  15.8 12.4 all_gather.38
  28.2 9.7 all_gather.39
  37.9 9.9 all_gather.37
  47.9 11.1 all_gather.40
  63.0 36.4 %all-gather.7.cloned.1.call-done = bf16[2048,1024]{1,0:T(8,128)(2,1)} async-done(((bf16[512,1024]{1,0:T(8,128)(2,1)}), bf16[2048,1024]{1,0:T(8,128)(2,1)}) %all-gather.7.cloned.1.call-update) | async-done | bytes 4194320 | tf_op jit(solution)/shard_map/all_gather | solution.py:30
  99.3 3.6 convolution_convert_fusion.1
  125.2 4.6 fusion.104
  129.8 7.5 fusion.116
  137.4 8.1 fusion
  145.5 7.6 fusion.103
  154.3 4.7 fusion.120
  159.6 142.6 %reduce-scatter.11.cloned.1.call-done = f32[512,1024]{1,0:T(8,128)} async-done(((f32[2048,1024]{1,0:T(8,128)}), f32[512,1024]{1,0:T(8,128)}) %reduce-scatter.11.cloned.1.call-update) | async-done | bytes 2097168 | tf_op jit(solution)/shard_map/reduce_scatter | solution.py:38
  310.9 80.5 %all-gather.9.cloned.1.call-done = bf16[2048,1024]{1,0:T(8,128)(2,1)} async-done(((bf16[512,1024]{1,0:T(8,128)(2,1)}), bf16[2048,1024]{1,0:T(8,128)(2,1)}) %all-gather.9.cloned.1.call-update) | async-done | bytes 4194320 | tf_op jit(solution)/shard_map/all_gather | solution.py:30
  391.4 10.6 fusion.121
  402.0 17.6 %all-gather.13.cloned.1.call-done = bf16[1024,1024]{1,0:T(8,128)(2,1)} async-done(((bf16[1024,128]{1,0:T(8,128)(2,1)}), bf16[1024,1024]{1,0:T(8,128)(2,1)}) %all-gather.13.cloned.1.call-update) | async-done | bytes 2097168 | tf_op jit(solution)/shard_map/all_gather | solution.py:164
  419.6 12.7 fusion.110
  432.4 144.6 %reduce-scatter.13.cloned.1.call-done = f32[512,1024]{1,0:T(8,128)} async-done(((f32[2048,1024]{1,0:T(8,128)}), f32[512,1024]{1,0:T(8,128)}) %reduce-scatter.13.cloned.1.call-update) | async-done | bytes 2097168 | tf_op jit(solution)/shard_map/reduce_scatter | solution.py:38
  586.8 81.0 %all-gather.15.cloned.1.call-done = bf16[2048,1024]{1,0:T(8,128)(2,1)} async-done(((bf16[512,1024]{1,0:T(8,128)(2,1)}), bf16[2048,1024]{1,0:T(8,128)(2,1)}) %all-gather.15.cloned.1.call-update) | async-done | bytes 4194320 | tf_op jit(solution)/shard_map/all_gather | solution.py:34
  667.8 12.6 fusion.10
  682.4 6.9 fusion.122
  689.4 143.1 %reduce-scatter.15.cloned.1.call-done = f32[512,1024]{1,0:T(8,128)} async-done(((f32[2048,1024]{1,0:T(8,128)}), f32[512,1024]{1,0:T(8,128)}) %reduce-scatter.15.cloned.1.call-update) | async-done | bytes 2097168 | tf_op jit(solution)/shard_map/reduce_scatter | solution.py:53
  841.6 81.2 %all-gather.17.cloned.1.call-done = bf16[2048,1024]{1,0:T(8,128)(2,1)} async-done(((bf16[512,1024]{1,0:T(8,128)(2,1)}), bf16[2048,1024]{1,0:T(8,128)(2,1)}) %all-gather.17.cloned.1.call-update) | async-done | bytes 4194320 | tf_op jit(solution)/shard_map/all_gather | solution.py:34
  922.9 3.6 convolution_convert_fusion
  932.3 4.4 multiply_reduce_fusion.2
  938.6 11.1 multiply_reduce_fusion.1
  949.7 6.3 fusion.44
  956.4 7.7 multiply_reduce_fusion
  964.1 3.8 fusion.50
  969.4 6.9 multiply_convert_fusion.2
  981.6 9.5 multiply_convert_fusion.1
  991.1 5.7 fusion.108
  998.0 10.4 multiply_convert_fusion
  1008.4 6.2 fusion.107
  1019.2 4.6 add_add_fusion
  1024.3 10.1 fusion.129
  1034.5 12.1 fusion.109
  1047.8 4.5 fusion.128
  1052.4 4.8 fusion.127
  1057.4 4.6 fusion.126
  1062.1 4.7 fusion.125
  1066.9 100.1 %reduce-scatter.17.cloned.1.call-done = f32[512,1024]{1,0:T(8,128)} async-done(((f32[2048,1024]{1,0:T(8,128)}), f32[512,1024]{1,0:T(8,128)}) %reduce-scatter.17.cloned.1.call-update) | async-done | bytes 2097168 | tf_op jit(solution)/shard_map/reduce_scatter | solution.py:53
  1169.7 41.8 %all-reduce.2 = (f32[4,1024]{1,0:T(4,128)}, f32[4,1024]{1,0:T(4,128)}) all-reduce(f32[4,1024]{1,0:T(4,128)S(1)} %pad_maximum_fusion.2, f32[4,1024]{1,0:T(4,128)S(1)} %pad_maximum_fusion.3), channel_id=1, replica_groups=mesh['wide'=8,'head'=4] {'wide','head'}, use_global_device_ids=true, to_apply=%region_42.43 | all-reduce | flops 8192 | bytes 65536 | tf_op jit(solution)/shard_map/psum | solution.py:225
  1215.1 7.6 reduce-scatter.27.cloned.1.call-done
  1222.7 54.7 %reduce-scatter.29.cloned.1.call-done = f32[1024,128]{1,0:T(8,128)} async-done(((f32[1024,1024]{1,0:T(8,128)}), f32[1024,128]{1,0:T(8,128)}) %reduce-scatter.29.cloned.1.call-update) | async-done | bytes 524304 | tf_op jit(solution)/shard_map/reduce_scatter | solution.py:223
  1277.5 39.5 %reduce-scatter.25.cloned.1.call-done = f32[256,128]{1,0:T(8,128)} async-done(((f32[256,1024]{1,0:T(8,128)}), f32[256,128]{1,0:T(8,128)}) %reduce-scatter.25.cloned.1.call-update) | async-done | bytes 131088 | tf_op jit(solution)/shard_map/reduce_scatter | solution.py:221
  1317.0 39.7 %reduce-scatter.23.cloned.1.call-done = f32[128,256]{1,0:T(8,128)} async-done(((f32[1024,256]{1,0:T(8,128)}), f32[128,256]{1,0:T(8,128)}) %reduce-scatter.23.cloned.1.call-update) | async-done | bytes 131088 | tf_op jit(solution)/shard_map/reduce_scatter | solution.py:220
  1356.7 39.5 %reduce-scatter.21.cloned.1.call-done = f32[128,256]{1,0:T(8,128)} async-done(((f32[1024,256]{1,0:T(8,128)}), f32[128,256]{1,0:T(8,128)}) %reduce-scatter.21.cloned.1.call-update) | async-done | bytes 131088 | tf_op jit(solution)/shard_map/reduce_scatter | solution.py:219
  1396.2 39.7 %reduce-scatter.19.cloned.1.call-done = f32[128,256]{1,0:T(8,128)} async-done(((f32[1024,256]{1,0:T(8,128)}), f32[128,256]{1,0:T(8,128)}) %reduce-scatter.19.cloned.1.call-update) | async-done | bytes 131088 | tf_op jit(solution)/shard_map/reduce_scatter | solution.py:218
  (291 shorter events, 93.5 us)
Async XLA Ops:
  8.0 20.2 %copy-start.61 = (bf16[128,256]{1,0:T(8,128)(2,1)S(1)}, bf16[128,256]{1,0:T(8,128)(2,1)}, u32[]{:S(2)}) copy-start(bf16[128,256]{1,0:T(8,128)(2,1)} %param.33) | copy-start | bytes 196612
  8.0 29.9 %copy-start.62 = (bf16[128,256]{1,0:T(8,128)(2,1)S(1)}, bf16[128,256]{1,0:T(8,128)(2,1)}, u32[]{:S(2)}) copy-start(bf16[128,256]{1,0:T(8,128)(2,1)} %param.34) | copy-start | bytes 196612
  8.0 39.8 %copy-start.63 = (bf16[256,128]{1,0:T(8,128)(2,1)S(1)}, bf16[256,128]{1,0:T(8,128)(2,1)}, u32[]{:S(2)}) copy-start(bf16[256,128]{1,0:T(8,128)(2,1)} %param.35) | copy-start | bytes 196612
  8.0 91.3 %all-gather.7.cloned.1.call-start = ((), (), s32[]{:S(2)}) async-start(), calls=%async_computation.10 | async-start | bytes 5242880 | tf_op jit(solution)/shard_map/all_gather | solution.py:30
  9.6 53.4 %copy-start.64 = (f32[512]{0:T(512)}, f32[512]{0:T(512)S(1)}, u32[]{:S(2)}) copy-start(f32[512]{0:T(512)S(1)} %broadcast_multiply_fusion.11) | copy-start | bytes 6148
  11.2 51.7 %copy-start.67 = (f32[512]{0:T(512)}, f32[512]{0:T(512)S(1)}, u32[]{:S(2)}) copy-start(f32[512]{0:T(512)S(1)} %add_rsqrt_fusion.3) | copy-start | bytes 6148
  15.7 286.6 %reduce-scatter.11.cloned.1.call-start = ((), (), s32[]{:S(2)}) async-start(), calls=%async_computation.11 | async-start | bytes 10485760 | tf_op jit(solution)/shard_map/reduce_scatter | solution.py:38
  37.9 65.0 %copy-start.42 = (bf16[1024,256]{1,0:T(8,128)(2,1)}, bf16[1024,256]{1,0:T(8,128)(2,1)S(1)}, u32[]{:S(2)}) copy-start(bf16[1024,256]{1,0:T(8,128)(2,1)S(1)} %all_gather.39) | copy-start | bytes 1572868
  103.0 26.9 %copy-start.13 = (bf16[2048,256]{0,1:T(8,128)(2,1)}, bf16[2048,256]{0,1:T(8,128)(2,1)S(1)}, u32[]{:S(2)}) copy-start(bf16[2048,256]{0,1:T(8,128)(2,1)S(1)} %convolution_convert_fusion.1) | copy-start | bytes 3145732
  103.2 15.0 %copy-start.19 = (bf16[1536,256]{0,1:T(8,128)(2,1)}, bf16[1536,256]{0,1:T(8,128)(2,1)S(1)}, u32[]{:S(2)}) copy-start(bf16[1536,256]{0,1:T(8,128)(2,1)S(1)} %slice.349) | copy-start | bytes 2359300
  104.5 41.0 %copy-start.15 = (bf16[2048,256]{0,1:T(8,128)(2,1)}, bf16[2048,256]{0,1:T(8,128)(2,1)S(1)}, u32[]{:S(2)}) copy-start(bf16[2048,256]{0,1:T(8,128)(2,1)S(1)} %convolution_convert_fusion.3) | copy-start | bytes 3145732
  107.2 11.0 copy-start.32
  107.2 22.7 %copy-start.26 = (bf16[512,256]{0,1:T(8,128)(2,1)}, bf16[512,256]{0,1:T(8,128)(2,1)S(1)}, u32[]{:S(2)}) copy-start(bf16[512,256]{0,1:T(8,128)(2,1)S(1)} %get-tuple-element.150) | copy-start | bytes 786436
  159.0 147.0 %copy-start.7 = (bf16[512,1024]{1,0:T(8,128)(2,1)S(1)}, bf16[512,1024]{1,0:T(8,128)(2,1)}, u32[]{:S(2)}) copy-start(bf16[512,1024]{1,0:T(8,128)(2,1)} %param.30) | copy-start | bytes 3145732
  159.0 151.9 %all-gather.11.cloned.1.call-start = ((), (), s32[]{:S(2)}) async-start(), calls=%async_computation.13 | async-start | bytes 2359296 | tf_op jit(solution)/shard_map/all_gather | solution.py:163
  159.6 231.8 %all-gather.9.cloned.1.call-start = ((), (), s32[]{:S(2)}) async-start(), calls=%async_computation.12 | async-start | bytes 5242880 | tf_op jit(solution)/shard_map/all_gather | solution.py:30
  310.1 109.6 %all-gather.13.cloned.1.call-start = ((), (), s32[]{:S(2)}) async-start(), calls=%async_computation.14 | async-start | bytes 2359296 | tf_op jit(solution)/shard_map/all_gather | solution.py:164
  310.7 266.4 %reduce-scatter.13.cloned.1.call-start = ((), (), s32[]{:S(2)}) async-start(), calls=%async_computation.15 | async-start | bytes 10485760 | tf_op jit(solution)/shard_map/reduce_scatter | solution.py:38
  432.3 148.6 %copy-start.17 = (bf16[512,1024]{1,0:T(8,128)(2,1)S(1)}, bf16[512,1024]{1,0:T(8,128)(2,1)}, u32[]{:S(2)}) copy-start(bf16[512,1024]{1,0:T(8,128)(2,1)} %param.31) | copy-start | bytes 3145732
  432.4 235.4 %all-gather.15.cloned.1.call-start = ((), (), s32[]{:S(2)}) async-start(), calls=%async_computation.16 | async-start | bytes 5242880 | tf_op jit(solution)/shard_map/all_gather | solution.py:34
  586.3 246.2 %reduce-scatter.15.cloned.1.call-start = ((), (), s32[]{:S(2)}) async-start(), calls=%async_computation.17 | async-start | bytes 10485760 | tf_op jit(solution)/shard_map/reduce_scatter | solution.py:53
  667.8 14.6 %copy-start.76 = (bf16[1024,1024]{1,0:T(8,128)(2,1)S(1)}, bf16[1024,1024]{1,0:T(8,128)(2,1)}, u32[]{:S(2)}) copy-start(bf16[1024,1024]{1,0:T(8,128)(2,1)} %all-gather.11.cloned.1.call-done) | copy-start | bytes 6291460
  689.4 233.5 %all-gather.17.cloned.1.call-start = ((), (), s32[]{:S(2)}) async-start(), calls=%async_computation.18 | async-start | bytes 5242880 | tf_op jit(solution)/shard_map/all_gather | solution.py:34
  838.6 84.3 %copy-start.47 = (bf16[256,1024]{1,0:T(8,128)(2,1)S(1)}, bf16[256,1024]{1,0:T(8,128)(2,1)}, u32[]{:S(2)}) copy-start(bf16[256,1024]{1,0:T(8,128)(2,1)} %all_gather.40) | copy-start | bytes 1572868
  841.5 325.5 %reduce-scatter.17.cloned.1.call-start = ((), (), s32[]{:S(2)}) async-start(), calls=%async_computation.19 | async-start | bytes 10485760 | tf_op jit(solution)/shard_map/reduce_scatter | solution.py:53
  938.5 17.5 %slice-start = ((s8[16777216]{0:T(1024)(128)(4,1)}), s8[4194304]{0:T(1024)(128)(4,1)S(1)}, s32[]{:S(2)}) async-start(s8[16777216]{0:T(1024)(128)(4,1)} %bitcast.166), calls=%async_computation.26 | async-start | bytes 8388608
  938.6 17.4 %slice-start.1 = ((s8[16777216]{0:T(1024)(128)(4,1)}), s8[4194304]{0:T(1024)(128)(4,1)S(1)}, s32[]{:S(2)}) async-start(s8[16777216]{0:T(1024)(128)(4,1)} %bitcast.166), calls=%async_computation.27 | async-start | bytes 8388608
  938.6 17.4 %slice-start.2 = ((s8[16777216]{0:T(1024)(128)(4,1)}), s8[4194304]{0:T(1024)(128)(4,1)S(1)}, s32[]{:S(2)}) async-start(s8[16777216]{0:T(1024)(128)(4,1)} %bitcast.166), calls=%async_computation.28 | async-start | bytes 8388608
  969.4 12.1 slice-start.4
  969.4 12.1 slice-start.5
  981.6 15.2 %copy-start.10 = (f32[2048,4,64]{0,2,1:T(8,128)S(1)}, f32[2048,4,64]{0,2,1:T(8,128)}, u32[]{:S(2)}) copy-start(f32[2048,4,64]{0,2,1:T(8,128)} %fusion.82) | copy-start | bytes 6291460
  1023.8 198.9 %reduce-scatter.27.cloned.1.call-start = ((), (), s32[]{:S(2)}) async-start(), calls=%async_computation.24 | async-start | bytes 4718592 | tf_op jit(solution)/shard_map/reduce_scatter | solution.py:222
  1034.4 243.1 %reduce-scatter.29.cloned.1.call-start = ((), (), s32[]{:S(2)}) async-start(), calls=%async_computation.25 | async-start | bytes 4718592 | tf_op jit(solution)/shard_map/reduce_scatter | solution.py:223
  1046.6 270.4 %reduce-scatter.25.cloned.1.call-start = ((), (), s32[]{:S(2)}) async-start(), calls=%async_computation.23 | async-start | bytes 1179648 | tf_op jit(solution)/shard_map/reduce_scatter | solution.py:221
  1052.3 304.4 %reduce-scatter.23.cloned.1.call-start = ((), (), s32[]{:S(2)}) async-start(), calls=%async_computation.22 | async-start | bytes 1179648 | tf_op jit(solution)/shard_map/reduce_scatter | solution.py:220
  1057.2 339.1 %reduce-scatter.21.cloned.1.call-start = ((), (), s32[]{:S(2)}) async-start(), calls=%async_computation.21 | async-start | bytes 1179648 | tf_op jit(solution)/shard_map/reduce_scatter | solution.py:219
  1062.0 105.0 %copy-start.8 = (bf16[512,1024]{1,0:T(8,128)(2,1)S(1)}, bf16[512,1024]{1,0:T(8,128)(2,1)}, u32[]{:S(2)}) copy-start(bf16[512,1024]{1,0:T(8,128)(2,1)} %param.30) | copy-start | bytes 3145732
  1062.0 105.0 %copy-start.59 = (f32[1,1024]{1,0:T(1,128)S(1)}, f32[1,1024]{1,0:T(1,128)}, u32[]{:S(2)}) copy-start(f32[1,1024]{1,0:T(1,128)} %copy-done.58) | copy-start | bytes 12292
  1062.1 105.0 %copy-start.65 = (f32[512]{0:T(512)S(1)}, f32[512]{0:T(512)}, u32[]{:S(2)}) copy-start(f32[512]{0:T(512)} %copy-done.64) | copy-start | bytes 6148
  1062.1 105.0 %copy-start.68 = (f32[512]{0:T(512)S(1)}, f32[512]{0:T(512)}, u32[]{:S(2)}) copy-start(f32[512]{0:T(512)} %copy-done.67) | copy-start | bytes 6148
  1062.1 373.9 %reduce-scatter.19.cloned.1.call-start = ((), (), s32[]{:S(2)}) async-start(), calls=%async_computation.20 | async-start | bytes 1179648 | tf_op jit(solution)/shard_map/reduce_scatter | solution.py:218
  1066.8 102.7 %copy-start.70 = (f32[1024]{0:T(1024)S(1)}, f32[1024]{0:T(1024)}, u32[]{:S(2)}) copy-start(f32[1024]{0:T(1024)} %get-tuple-element.128) | copy-start | bytes 12292
  1066.8 102.8 %copy-start.72 = (f32[1024]{0:T(1024)S(1)}, f32[1024]{0:T(1024)}, u32[]{:S(2)}) copy-start(f32[1024]{0:T(1024)} %get-tuple-element.124) | copy-start | bytes 12292
  1066.8 102.8 %copy-start.74 = (f32[1024]{0:T(1024)S(1)}, f32[1024]{0:T(1024)}, u32[]{:S(2)}) copy-start(f32[1024]{0:T(1024)} %get-tuple-element.122) | copy-start | bytes 12292
  1066.8 102.8 %copy-start.69 = (f32[1024]{0:T(1024)S(1)}, f32[1024]{0:T(1024)}, u32[]{:S(2)}) copy-start(f32[1024]{0:T(1024)} %get-tuple-element.137) | copy-start | bytes 12292
  1066.8 102.8 %copy-start.71 = (f32[1024]{0:T(1024)S(1)}, f32[1024]{0:T(1024)}, u32[]{:S(2)}) copy-start(f32[1024]{0:T(1024)} %get-tuple-element.135) | copy-start | bytes 12292
  1066.8 102.8 %copy-start.73 = (f32[1024]{0:T(1024)S(1)}, f32[1024]{0:T(1024)}, u32[]{:S(2)}) copy-start(f32[1024]{0:T(1024)} %get-tuple-element.134) | copy-start | bytes 12292
  1066.8 144.7 %copy-start.12 = (f32[512,1024]{1,0:T(8,128)S(1)}, f32[512,1024]{1,0:T(8,128)}, u32[]{:S(2)}) copy-start(f32[512,1024]{1,0:T(8,128)} %copy-done.11) | copy-start | bytes 6291460
  (55 other events, 218.1 us)
Sparse Core Ops, SparseCore 0:
  15.8 83.4 all-gather.6
  159.1 143.0 reduce-scatter.10
  586.4 81.2 all-gather.14
  689.5 143.0 reduce-scatter.14
Sparse Core Ops, SparseCore 1:
  161.4 26.1 all-gather.10
  310.2 81.2 all-gather.8
  393.2 26.4 all-gather.12
  432.4 144.6 reduce-scatter.12
  841.6 81.2 all-gather.16
  1023.9 143.1 reduce-scatter.16
  1170.8 51.9 reduce-scatter.26
  1226.5 50.9 reduce-scatter.28
  1281.1 35.9 reduce-scatter.24
  1320.8 35.9 reduce-scatter.22
  1360.3 35.9 reduce-scatter.20
  1400.0 35.9 reduce-scatter.18
where the time goes:
time: 1450 us; the launch traced here: 1440 us
  waiting for transfers between devices  1050 us (72%)
  matrix products  193 us (13%)
  blocking collectives  85 us (6%)
  other arithmetic  81.8 us (6%)
  between operations  16.8 us (1%)
  local copies, waits for them, and re-layouts  15.2 us (1%)
    reduce_scatter x2, waiting for transfers between devices, branch_sum(): lax.psum_scatter(jnp.dot(left_op, right_op, preferred_element_type=jnp.fl...  287 us
    reduce_scatter x2, waiting for transfers between devices, input_sum(): return lax.psum_scatter(summed, 'head', scatter_dimension=0, tiled=True)  243 us
    all_gather x2, waiting for transfers between devices, grads_in(): return lax.all_gather(values, 'head', axis=0, tiled=True)  162 us
    all_gather x2, waiting for transfers between devices, rows_in(): return lax.all_gather(values, 'head', axis=0, tiled=True)  117 us
    reduce_scatter x1, waiting for transfers between devices, on_device(): lax.psum_scatter(grad_down, 'wide', scatter_dimension=1, tiled=True)  54.7 us
    psum x1, blocking collectives, on_device(): lax.psum((jnp.stack([gain_a, gain_z, gain_c, gain_m]), jnp.stack([bias_a,...  41.8 us
    dot_general x6, matrix products, contract_rows(): lax.dot_general(left_op, right_op, (((0,), (0,)), ((), ())), preferred_el...  40.8 us
    reduce_scatter x1, waiting for transfers between devices, on_device(): lax.psum_scatter(grad_v, 'wide', scatter_dimension=0, tiled=True)  39.7 us
  transfers between devices with their start and end apart: 16, of which 15 were waited for; matrix products, arithmetic and copies ran while one was open for 5% of the time, Pallas kernels for 0%

commit v1 on v0

--- a/solution.py
+++ b/solution.py
@@ -6,6 +6,28 @@
 
 HD = 64
 EPS = 1e-05
+
+
+def laid_out(blocks, dim):
+    shape = list(blocks.shape[1:])
+    shape[dim] *= blocks.shape[0]
+    return jnp.moveaxis(blocks, 0, dim).reshape(shape)
+
+
+def ring_gather(array, axis, dim):
+    size = lax.axis_size(axis)
+    pairs = [(i, (i + 1) % size) for i in range(size)]
+    back = [(b, a) for a, b in pairs]
+    lower, upper = ([], [])
+    for step in range(size - 1):
+        if step % 2 == 0:
+            lower.append(lax.ppermute(lower[-1] if lower else array, axis, pairs))
+        else:
+            upper.append(lax.ppermute(upper[-1] if upper else array, axis, back))
+    blocks = jnp.stack([*lower[::-1], array, *upper])
+    shift = lax.axis_index(axis) - len(lower)
+    blocks = blocks[(jnp.arange(size) - shift) % size]
+    return laid_out(blocks, dim)
 
 
 def normalize(values, gain, bias):
@@ -27,7 +49,7 @@
 
 
 def rows_in(values):
-    return lax.all_gather(values, "head", axis=0, tiled=True)
+    return ring_gather(values, "head", 0)
 
 
 def grads_in(values):

time: 1450 us -> 1430 us (0.986)
  waiting for transfers between devices: 1050 us -> 984 us
  starting transfers between devices: 1.84 us -> 34.1 us
    all_gather x2 -> x0, waiting for transfers between devices: 117 us -> none  [rows_in(): return lax.all_gather(values, 'head', axis=0, tiled=True)]
    ppermute x0 -> x6, waiting for transfers between devices: none -> 69.4 us  [the longest x4 68.8 us: ring_gather(): lower.append(lax.ppermute(lower[-1] if lower else array, axis, pairs))]
    ppermute x0 -> x6, starting transfers between devices: none -> 32.5 us  [the longest x4 24.6 us: ring_gather(): lower.append(lax.ppermute(lower[-1] if lower else array, axis, pairs))]
    all_gather x1, waiting for transfers between devices: 17.6 us -> 0.01 us  [on_device(): lax.all_gather(w_down, 'wide', axis=1, tiled=True)]
  transfers between devices with their start and end apart: 16 -> 20, of which waited for: 15 -> 17; matrix products, arithmetic and copies ran while one was open for 5% -> 5% of each run, Pallas kernels for 0% -> 0%
where the time goes in v1:
time: 1430 us
  waiting for transfers between devices  984 us (69%)
  matrix products  193 us (13%)
  other arithmetic  87.8 us (6%)
  blocking collectives  83.3 us (6%)
  starting transfers between devices  34.1 us (2%)
  local copies, waits for them, and re-layouts  25.9 us (2%)
  between operations  17.2 us (1%)
    reduce_scatter x2, waiting for transfers between devices, branch_sum(): lax.psum_scatter(jnp.dot(left_op, right_op, preferred_element_type=jnp.fl...  285 us
    reduce_scatter x2, waiting for transfers between devices, input_sum(): return lax.psum_scatter(summed, 'head', scatter_dimension=0, tiled=True)  244 us
    all_gather x2, waiting for transfers between devices, grads_in(): return lax.all_gather(values, 'head', axis=0, tiled=True)  162 us
    ppermute x4, waiting for transfers between devices, ring_gather(): lower.append(lax.ppermute(lower[-1] if lower else array, axis, pairs))  68.8 us
    reduce_scatter x1, waiting for transfers between devices, on_device(): lax.psum_scatter(grad_down, 'wide', scatter_dimension=1, tiled=True)  55 us
    psum x1, blocking collectives, on_device(): lax.psum((jnp.stack([gain_a, gain_z, gain_c, gain_m]), jnp.stack([bias_a,...  41.9 us
    dot_general x6, matrix products, contract_rows(): lax.dot_general(left_op, right_op, (((0,), (0,)), ((), ())), preferred_el...  40.5 us
    reduce_scatter x1, waiting for transfers between devices, on_device(): lax.psum_scatter(grad_o, 'wide', scatter_dimension=1, tiled=True)  39.8 us
  transfers between devices with their start and end apart: 20, of which 17 were waited for; matrix products, arithmetic and copies ran while one was open for 5% of the time, Pallas kernels for 0%

profile of v1, /device:TPU:0, one launch (start us, length us, event | category | flops | bytes accessed | tf_op | source)
XLA Modules:
  0.0 1425.2 jit_solution(17862721521302118122)
XLA Ops:
  15.7 5.1 collective-permute-start.2
  20.9 10.9 all_gather.31
  31.8 9.7 all_gather.32
  41.5 9.9 all_gather.30
  51.5 10.8 all_gather.33
  72.1 21.4 %collective-permute-done.1 = bf16[512,1024]{1,0:T(8,128)(2,1)S(1)} collective-permute-done((bf16[512,1024]{1,0:T(8,128)(2,1)}, bf16[512,1024]{1,0:T(8,128)(2,1)S(1)}, u32[]{:S(2)}, u32[]{:S(2)}) %collective-permute-start.1) | collective-permute-done | bytes 1048608 | tf_op jit(solution)/shard_map/ppermute | solution.py:24
  96.9 5.0 gather_fusion
  128.0 4.7 fusion.102
  132.7 7.5 fusion.123
  140.3 8.1 fusion
  148.5 8.0 fusion.101
  157.7 4.6 fusion.127
  163.5 141.8 %reduce-scatter.11.cloned.1.call-done = f32[512,1024]{1,0:T(8,128)} async-done(((f32[2048,1024]{1,0:T(8,128)}), f32[512,1024]{1,0:T(8,128)}) %reduce-scatter.11.cloned.1.call-update) | async-done | bytes 2097168 | tf_op jit(solution)/shard_map/reduce_scatter | solution.py:60
  316.0 24.0 %collective-permute-done.3 = bf16[512,1024]{1,0:T(8,128)(2,1)S(1)} collective-permute-done((bf16[512,1024]{1,0:T(8,128)(2,1)S(1)}, bf16[512,1024]{1,0:T(8,128)(2,1)S(1)}, u32[]{:S(2)}, u32[]{:S(2)}) %collective-permute-start.3) | collective-permute-done | bytes 1048608 | tf_op jit(solution)/shard_map/ppermute | solution.py:24
  340.0 21.4 %collective-permute-start.4 = (bf16[512,1024]{1,0:T(8,128)(2,1)S(1)}, bf16[512,1024]{1,0:T(8,128)(2,1)S(1)}, u32[]{:S(2)}, u32[]{:S(2)}) collective-permute-start(bf16[512,1024]{1,0:T(8,128)(2,1)S(1)} %collective-permute-done.3), channel_id=1, source_target_pairs={{0,1},{1,2},{2,3},{3,0},{4,5},{5,6},{6,7},{7,4},{8,9},{9,10},{10,1... | collective-permute-start | bytes 3145736 | tf_op jit(solution)/shard_map/ppermute | solution.py:24
  362.4 21.0 %collective-permute-done.4 = bf16[512,1024]{1,0:T(8,128)(2,1)S(1)} collective-permute-done((bf16[512,1024]{1,0:T(8,128)(2,1)S(1)}, bf16[512,1024]{1,0:T(8,128)(2,1)S(1)}, u32[]{:S(2)}, u32[]{:S(2)}) %collective-permute-start.4) | collective-permute-done | bytes 1048608 | tf_op jit(solution)/shard_map/ppermute | solution.py:24
  385.7 5.0 gather_fusion.1
  390.7 10.6 fusion.128
  401.3 12.7 fusion.117
  414.2 143.6 %reduce-scatter.13.cloned.1.call-done = f32[512,1024]{1,0:T(8,128)} async-done(((f32[2048,1024]{1,0:T(8,128)}), f32[512,1024]{1,0:T(8,128)}) %reduce-scatter.13.cloned.1.call-update) | async-done | bytes 2097168 | tf_op jit(solution)/shard_map/reduce_scatter | solution.py:60
  567.2 81.5 %all-gather.9.cloned.1.call-done = bf16[2048,1024]{1,0:T(8,128)(2,1)} async-done(((bf16[512,1024]{1,0:T(8,128)(2,1)}), bf16[2048,1024]{1,0:T(8,128)(2,1)}) %all-gather.9.cloned.1.call-update) | async-done | bytes 4194320 | tf_op jit(solution)/shard_map/all_gather | solution.py:56
  648.6 12.6 fusion.10
  663.2 7.0 fusion.129
  670.3 143.2 %reduce-scatter.15.cloned.1.call-done = f32[512,1024]{1,0:T(8,128)} async-done(((f32[2048,1024]{1,0:T(8,128)}), f32[512,1024]{1,0:T(8,128)}) %reduce-scatter.15.cloned.1.call-update) | async-done | bytes 2097168 | tf_op jit(solution)/shard_map/reduce_scatter | solution.py:75
  823.0 81.0 %all-gather.11.cloned.1.call-done = bf16[2048,1024]{1,0:T(8,128)(2,1)} async-done(((bf16[512,1024]{1,0:T(8,128)(2,1)}), bf16[2048,1024]{1,0:T(8,128)(2,1)}) %all-gather.11.cloned.1.call-update) | async-done | bytes 4194320 | tf_op jit(solution)/shard_map/all_gather | solution.py:56
  919.5 11.1 multiply_reduce_fusion.1
  930.6 6.3 fusion.44
  937.3 7.7 multiply_reduce_fusion
  950.4 6.9 multiply_convert_fusion.2
  962.6 9.5 multiply_convert_fusion.1
  972.2 4.9 fusion.93
  978.4 10.4 multiply_convert_fusion
  988.8 6.2 fusion.94
  999.6 4.7 add_add_fusion
  1004.6 10.1 fusion.135
  1014.8 12.1 fusion.116
  1028.1 4.5 fusion.134
  1032.7 4.6 fusion.133
  1037.7 4.6 fusion.132
  1042.4 4.7 fusion.105
  1047.1 100.5 %reduce-scatter.17.cloned.1.call-done = f32[512,1024]{1,0:T(8,128)} async-done(((f32[2048,1024]{1,0:T(8,128)}), f32[512,1024]{1,0:T(8,128)}) %reduce-scatter.17.cloned.1.call-update) | async-done | bytes 2097168 | tf_op jit(solution)/shard_map/reduce_scatter | solution.py:75
  1150.3 41.9 %all-reduce.2 = (f32[4,1024]{1,0:T(4,128)}, f32[4,1024]{1,0:T(4,128)}) all-reduce(f32[4,1024]{1,0:T(4,128)S(1)} %pad_maximum_fusion.4, f32[4,1024]{1,0:T(4,128)S(1)} %pad_maximum_fusion.5), channel_id=1, replica_groups=mesh['wide'=8,'head'=4] {'wide','head'}, use_global_device_ids=true, to_apply=%region_42.43 | all-reduce | flops 8192 | bytes 65536 | tf_op jit(solution)/shard_map/psum | solution.py:247
  1195.8 7.9 reduce-scatter.27.cloned.1.call-done
  1203.7 55.0 %reduce-scatter.29.cloned.1.call-done = f32[1024,128]{1,0:T(8,128)} async-done(((f32[1024,1024]{1,0:T(8,128)}), f32[1024,128]{1,0:T(8,128)}) %reduce-scatter.29.cloned.1.call-update) | async-done | bytes 524304 | tf_op jit(solution)/shard_map/reduce_scatter | solution.py:245
  1258.8 39.8 %reduce-scatter.25.cloned.1.call-done = f32[256,128]{1,0:T(8,128)} async-done(((f32[256,1024]{1,0:T(8,128)}), f32[256,128]{1,0:T(8,128)}) %reduce-scatter.25.cloned.1.call-update) | async-done | bytes 131088 | tf_op jit(solution)/shard_map/reduce_scatter | solution.py:243
  1298.5 39.6 %reduce-scatter.23.cloned.1.call-done = f32[128,256]{1,0:T(8,128)} async-done(((f32[1024,256]{1,0:T(8,128)}), f32[128,256]{1,0:T(8,128)}) %reduce-scatter.23.cloned.1.call-update) | async-done | bytes 131088 | tf_op jit(solution)/shard_map/reduce_scatter | solution.py:242
  1338.1 39.8 %reduce-scatter.21.cloned.1.call-done = f32[128,256]{1,0:T(8,128)} async-done(((f32[1024,256]{1,0:T(8,128)}), f32[128,256]{1,0:T(8,128)}) %reduce-scatter.21.cloned.1.call-update) | async-done | bytes 131088 | tf_op jit(solution)/shard_map/reduce_scatter | solution.py:241
  1377.9 39.6 %reduce-scatter.19.cloned.1.call-done = f32[128,256]{1,0:T(8,128)} async-done(((f32[1024,256]{1,0:T(8,128)}), f32[128,256]{1,0:T(8,128)}) %reduce-scatter.19.cloned.1.call-update) | async-done | bytes 131088 | tf_op jit(solution)/shard_map/reduce_scatter | solution.py:240
  (315 shorter events, 124.4 us)
Async XLA Ops:
  8.0 56.2 %copy-start.7 = (bf16[512,1024]{1,0:T(8,128)(2,1)S(1)}, bf16[512,1024]{1,0:T(8,128)(2,1)}, u32[]{:S(2)}) copy-start(bf16[512,1024]{1,0:T(8,128)(2,1)} %param.30) | copy-start | bytes 3145732
  8.0 23.7 %copy-start.69 = (bf16[128,256]{1,0:T(8,128)(2,1)S(1)}, bf16[128,256]{1,0:T(8,128)(2,1)}, u32[]{:S(2)}) copy-start(bf16[128,256]{1,0:T(8,128)(2,1)} %param.33) | copy-start | bytes 196612
  8.0 33.5 %copy-start.70 = (bf16[128,256]{1,0:T(8,128)(2,1)S(1)}, bf16[128,256]{1,0:T(8,128)(2,1)}, u32[]{:S(2)}) copy-start(bf16[128,256]{1,0:T(8,128)(2,1)} %param.34) | copy-start | bytes 196612
  8.1 43.4 %copy-start.71 = (bf16[256,128]{1,0:T(8,128)(2,1)S(1)}, bf16[256,128]{1,0:T(8,128)(2,1)}, u32[]{:S(2)}) copy-start(bf16[256,128]{1,0:T(8,128)(2,1)} %param.35) | copy-start | bytes 196612
  8.1 297.2 %reduce-scatter.11.cloned.1.call-start = ((), (), s32[]{:S(2)}) async-start(), calls=%async_computation.10 | async-start | bytes 10485760 | tf_op jit(solution)/shard_map/reduce_scatter | solution.py:60
  9.6 55.0 %copy-start.66 = (f32[512]{0:T(512)}, f32[512]{0:T(512)S(1)}, u32[]{:S(2)}) copy-start(f32[512]{0:T(512)S(1)} %broadcast_multiply_fusion.11) | copy-start | bytes 6148
  11.3 60.8 %copy-start.72 = (f32[512]{0:T(512)}, f32[512]{0:T(512)S(1)}, u32[]{:S(2)}) copy-start(f32[512]{0:T(512)S(1)} %add_rsqrt_fusion.3) | copy-start | bytes 6148
  12.2 59.9 %copy-start.64 = (f32[1,1024]{1,0:T(1,128)}, f32[1,1024]{1,0:T(1,128)S(1)}, u32[]{:S(2)}) copy-start(f32[1,1024]{1,0:T(1,128)S(1)} %get-tuple-element.155) | copy-start | bytes 12292
  15.7 56.3 %collective-permute-start.2 = (bf16[512,1024]{1,0:T(8,128)(2,1)}, bf16[512,1024]{1,0:T(8,128)(2,1)}, u32[]{:S(2)}, u32[]{:S(2)}) collective-permute-start(bf16[512,1024]{1,0:T(8,128)(2,1)} %fusion.61), channel_id=1, source_target_pairs={{1,0},{2,1},{3,2},{0,3},{5,4},{6,5},{7,6},{4,7},{9,8},{10,9},{11,1... | collective-permute-start | bytes 3145736 | tf_op jit(solution)/shard_map/ppermute | solution.py:26
  20.8 46.1 %collective-permute-start = (bf16[512,1024]{1,0:T(8,128)(2,1)}, bf16[512,1024]{1,0:T(8,128)(2,1)}, u32[]{:S(2)}, u32[]{:S(2)}) collective-permute-start(bf16[512,1024]{1,0:T(8,128)(2,1)} %fusion.61), channel_id=1, source_target_pairs={{0,1},{1,2},{2,3},{3,0},{4,5},{5,6},{6,7},{7,4},{8,9},{9,10},{10,1... | collective-permute-start | bytes 3145736 | tf_op jit(solution)/shard_map/ppermute | solution.py:24
  41.5 60.4 %copy-start.44 = (bf16[1024,256]{1,0:T(8,128)(2,1)}, bf16[1024,256]{1,0:T(8,128)(2,1)S(1)}, u32[]{:S(2)}) copy-start(bf16[1024,256]{1,0:T(8,128)(2,1)S(1)} %all_gather.32) | copy-start | bytes 1572868
  66.9 26.6 %collective-permute-start.1 = (bf16[512,1024]{1,0:T(8,128)(2,1)}, bf16[512,1024]{1,0:T(8,128)(2,1)S(1)}, u32[]{:S(2)}, u32[]{:S(2)}) collective-permute-start(bf16[512,1024]{1,0:T(8,128)(2,1)} %collective-permute-done), channel_id=1, source_target_pairs={{0,1},{1,2},{2,3},{3,0},{4,5},{5,6},{6,7},{7,4},{8,9},{9,10},{10,1... | collective-permute-start | bytes 3145736 | tf_op jit(solution)/shard_map/ppermute | solution.py:24
  105.5 27.2 %copy-start.13 = (bf16[2048,256]{0,1:T(8,128)(2,1)}, bf16[2048,256]{0,1:T(8,128)(2,1)S(1)}, u32[]{:S(2)}) copy-start(bf16[2048,256]{0,1:T(8,128)(2,1)S(1)} %convolution_convert_fusion.1) | copy-start | bytes 3145732
  107.1 41.4 %copy-start.15 = (bf16[2048,256]{0,1:T(8,128)(2,1)}, bf16[2048,256]{0,1:T(8,128)(2,1)S(1)}, u32[]{:S(2)}) copy-start(bf16[2048,256]{0,1:T(8,128)(2,1)S(1)} %convolution_convert_fusion.3) | copy-start | bytes 3145732
  109.8 23.0 %copy-start.28 = (bf16[512,256]{0,1:T(8,128)(2,1)}, bf16[512,256]{0,1:T(8,128)(2,1)S(1)}, u32[]{:S(2)}) copy-start(bf16[512,256]{0,1:T(8,128)(2,1)S(1)} %get-tuple-element.150) | copy-start | bytes 786436
  162.3 228.4 %all-gather.5.cloned.1.call-start = ((), (), s32[]{:S(2)}) async-start(), calls=%async_computation.11 | async-start | bytes 2359296 | tf_op jit(solution)/shard_map/all_gather | solution.py:185
  162.9 238.4 %all-gather.7.cloned.1.call-start = ((), (), s32[]{:S(2)}) async-start(), calls=%async_computation.12 | async-start | bytes 2359296 | tf_op jit(solution)/shard_map/all_gather | solution.py:186
  163.5 394.4 %reduce-scatter.13.cloned.1.call-start = ((), (), s32[]{:S(2)}) async-start(), calls=%async_computation.13 | async-start | bytes 10485760 | tf_op jit(solution)/shard_map/reduce_scatter | solution.py:60
  312.1 27.9 %collective-permute-start.3 = (bf16[512,1024]{1,0:T(8,128)(2,1)S(1)}, bf16[512,1024]{1,0:T(8,128)(2,1)S(1)}, u32[]{:S(2)}, u32[]{:S(2)}) collective-permute-start(bf16[512,1024]{1,0:T(8,128)(2,1)S(1)} %add_convert_fusion.1), channel_id=1, source_target_pairs={{0,1},{1,2},{2,3},{3,0},{4,5},{5,6},{6,7},{7,4},{8,9},{9,10},{10,1... | collective-permute-start | bytes 3145736 | tf_op jit(solution)/shard_map/ppermute | solution.py:24
  313.2 49.2 %collective-permute-start.5 = (bf16[512,1024]{1,0:T(8,128)(2,1)S(1)}, bf16[512,1024]{1,0:T(8,128)(2,1)S(1)}, u32[]{:S(2)}, u32[]{:S(2)}) collective-permute-start(bf16[512,1024]{1,0:T(8,128)(2,1)S(1)} %add_convert_fusion.1), channel_id=1, source_target_pairs={{1,0},{2,1},{3,2},{0,3},{5,4},{6,5},{7,6},{4,7},{9,8},{10,9},{11,1... | collective-permute-start | bytes 3145736 | tf_op jit(solution)/shard_map/ppermute | solution.py:26
  340.0 43.4 %collective-permute-start.4 = (bf16[512,1024]{1,0:T(8,128)(2,1)S(1)}, bf16[512,1024]{1,0:T(8,128)(2,1)S(1)}, u32[]{:S(2)}, u32[]{:S(2)}) collective-permute-start(bf16[512,1024]{1,0:T(8,128)(2,1)S(1)} %collective-permute-done.3), channel_id=1, source_target_pairs={{0,1},{1,2},{2,3},{3,0},{4,5},{5,6},{6,7},{7,4},{8,9},{9,10},{10,1... | collective-permute-start | bytes 3145736 | tf_op jit(solution)/shard_map/ppermute | solution.py:24
  414.0 147.8 %copy-start.17 = (bf16[512,1024]{1,0:T(8,128)(2,1)S(1)}, bf16[512,1024]{1,0:T(8,128)(2,1)}, u32[]{:S(2)}) copy-start(bf16[512,1024]{1,0:T(8,128)(2,1)} %param.31) | copy-start | bytes 3145732
  414.0 234.6 %all-gather.9.cloned.1.call-start = ((), (), s32[]{:S(2)}) async-start(), calls=%async_computation.14 | async-start | bytes 5242880 | tf_op jit(solution)/shard_map/all_gather | solution.py:56
  567.1 246.4 %reduce-scatter.15.cloned.1.call-start = ((), (), s32[]{:S(2)}) async-start(), calls=%async_computation.15 | async-start | bytes 10485760 | tf_op jit(solution)/shard_map/reduce_scatter | solution.py:75
  670.2 233.7 %all-gather.11.cloned.1.call-start = ((), (), s32[]{:S(2)}) async-start(), calls=%async_computation.16 | async-start | bytes 5242880 | tf_op jit(solution)/shard_map/all_gather | solution.py:56
  819.5 84.4 %copy-start.47 = (bf16[256,1024]{1,0:T(8,128)(2,1)S(1)}, bf16[256,1024]{1,0:T(8,128)(2,1)}, u32[]{:S(2)}) copy-start(bf16[256,1024]{1,0:T(8,128)(2,1)} %all_gather.33) | copy-start | bytes 1572868
  822.4 325.2 %reduce-scatter.17.cloned.1.call-start = ((), (), s32[]{:S(2)}) async-start(), calls=%async_computation.17 | async-start | bytes 10485760 | tf_op jit(solution)/shard_map/reduce_scatter | solution.py:75
  919.5 17.4 %slice-start = ((s8[16777216]{0:T(1024)(128)(4,1)}), s8[4194304]{0:T(1024)(128)(4,1)S(1)}, s32[]{:S(2)}) async-start(s8[16777216]{0:T(1024)(128)(4,1)} %bitcast.183), calls=%async_computation.24 | async-start | bytes 8388608
  919.5 17.4 %slice-start.1 = ((s8[16777216]{0:T(1024)(128)(4,1)}), s8[4194304]{0:T(1024)(128)(4,1)S(1)}, s32[]{:S(2)}) async-start(s8[16777216]{0:T(1024)(128)(4,1)} %bitcast.183), calls=%async_computation.25 | async-start | bytes 8388608
  919.5 17.4 %slice-start.2 = ((s8[16777216]{0:T(1024)(128)(4,1)}), s8[4194304]{0:T(1024)(128)(4,1)S(1)}, s32[]{:S(2)}) async-start(s8[16777216]{0:T(1024)(128)(4,1)} %bitcast.183), calls=%async_computation.26 | async-start | bytes 8388608
  977.2 20.9 %copy-start.57 = (bf16[4,64,512]{2,1,0:T(8,128)(2,1)}, bf16[4,64,512]{2,1,0:T(8,128)(2,1)S(1)}, u32[]{:S(2)}) copy-start(bf16[4,64,512]{2,1,0:T(8,128)(2,1)S(1)} %fusion.93) | copy-start | bytes 786436
  1004.4 199.4 %reduce-scatter.27.cloned.1.call-start = ((), (), s32[]{:S(2)}) async-start(), calls=%async_computation.22 | async-start | bytes 4718592 | tf_op jit(solution)/shard_map/reduce_scatter | solution.py:244
  1014.7 244.0 %reduce-scatter.29.cloned.1.call-start = ((), (), s32[]{:S(2)}) async-start(), calls=%async_computation.23 | async-start | bytes 4718592 | tf_op jit(solution)/shard_map/reduce_scatter | solution.py:245
  1026.9 271.6 %reduce-scatter.25.cloned.1.call-start = ((), (), s32[]{:S(2)}) async-start(), calls=%async_computation.21 | async-start | bytes 1179648 | tf_op jit(solution)/shard_map/reduce_scatter | solution.py:243
  1032.7 305.4 %reduce-scatter.23.cloned.1.call-start = ((), (), s32[]{:S(2)}) async-start(), calls=%async_computation.20 | async-start | bytes 1179648 | tf_op jit(solution)/shard_map/reduce_scatter | solution.py:242
  1037.4 340.5 %reduce-scatter.21.cloned.1.call-start = ((), (), s32[]{:S(2)}) async-start(), calls=%async_computation.19 | async-start | bytes 1179648 | tf_op jit(solution)/shard_map/reduce_scatter | solution.py:241
  1042.2 375.2 %reduce-scatter.19.cloned.1.call-start = ((), (), s32[]{:S(2)}) async-start(), calls=%async_computation.18 | async-start | bytes 1179648 | tf_op jit(solution)/shard_map/reduce_scatter | solution.py:240
  1042.3 105.3 %copy-start.8 = (bf16[512,1024]{1,0:T(8,128)(2,1)S(1)}, bf16[512,1024]{1,0:T(8,128)(2,1)}, u32[]{:S(2)}) copy-start(bf16[512,1024]{1,0:T(8,128)(2,1)} %param.30) | copy-start | bytes 3145732
  1042.3 105.3 %copy-start.65 = (f32[1,1024]{1,0:T(1,128)S(1)}, f32[1,1024]{1,0:T(1,128)}, u32[]{:S(2)}) copy-start(f32[1,1024]{1,0:T(1,128)} %copy-done.64) | copy-start | bytes 12292
  1042.3 105.3 %copy-start.67 = (f32[512]{0:T(512)S(1)}, f32[512]{0:T(512)}, u32[]{:S(2)}) copy-start(f32[512]{0:T(512)} %copy-done.66) | copy-start | bytes 6148
  1042.4 105.3 %copy-start.73 = (f32[512]{0:T(512)S(1)}, f32[512]{0:T(512)}, u32[]{:S(2)}) copy-start(f32[512]{0:T(512)} %copy-done.72) | copy-start | bytes 6148
  1047.0 103.2 %copy-start.76 = (f32[1024]{0:T(1024)S(1)}, f32[1024]{0:T(1024)}, u32[]{:S(2)}) copy-start(f32[1024]{0:T(1024)} %get-tuple-element.128) | copy-start | bytes 12292
  1047.0 103.2 %copy-start.78 = (f32[1024]{0:T(1024)S(1)}, f32[1024]{0:T(1024)}, u32[]{:S(2)}) copy-start(f32[1024]{0:T(1024)} %get-tuple-element.124) | copy-start | bytes 12292
  1047.0 103.2 %copy-start.80 = (f32[1024]{0:T(1024)S(1)}, f32[1024]{0:T(1024)}, u32[]{:S(2)}) copy-start(f32[1024]{0:T(1024)} %get-tuple-element.122) | copy-start | bytes 12292
  1047.0 103.2 %copy-start.75 = (f32[1024]{0:T(1024)S(1)}, f32[1024]{0:T(1024)}, u32[]{:S(2)}) copy-start(f32[1024]{0:T(1024)} %get-tuple-element.137) | copy-start | bytes 12292
  1047.0 103.2 %copy-start.77 = (f32[1024]{0:T(1024)S(1)}, f32[1024]{0:T(1024)}, u32[]{:S(2)}) copy-start(f32[1024]{0:T(1024)} %get-tuple-element.135) | copy-start | bytes 12292
  1047.0 103.2 %copy-start.79 = (f32[1024]{0:T(1024)S(1)}, f32[1024]{0:T(1024)}, u32[]{:S(2)}) copy-start(f32[1024]{0:T(1024)} %get-tuple-element.134) | copy-start | bytes 12292
  1047.0 145.2 %copy-start.12 = (f32[512,1024]{1,0:T(8,128)S(1)}, f32[512,1024]{1,0:T(8,128)}, u32[]{:S(2)}) copy-start(f32[512,1024]{1,0:T(8,128)} %copy-done.11) | copy-start | bytes 6291460
  (64 other events, 323.7 us)
Sparse Core Ops, SparseCore 0:
  162.4 142.8 reduce-scatter.10
  414.1 143.7 reduce-scatter.12
  567.2 81.3 all-gather.8
  670.4 143.0 reduce-scatter.14
  822.6 81.3 all-gather.10
  1004.5 143.0 reduce-scatter.16
  1151.6 52.1 reduce-scatter.26
  1207.7 51.0 reduce-scatter.28
  1262.5 35.9 reduce-scatter.24
  1302.1 35.9 reduce-scatter.22
  1341.9 35.9 reduce-scatter.20
  1381.5 35.9 reduce-scatter.18
Sparse Core Ops, SparseCore 1:
  164.7 25.8 all-gather.4
  192.3 27.9 all-gather.6
